TPU v7x, 32 devices: a whole 2x2x4 slice. The times are simulated.
32 devices in a mesh: dp: 8 (over y, x, core), tensor: 4 (over z).
Axes of the slice: x: 2, y: 2, z: 4, core: 2. Of those that a mesh axis runs over, the one named last changes fastest.
Arguments:
- tokens: bfloat16 [8192, 1024], P(('dp', 'tensor')), may hold values from -6 to 6
- block_ids: int32 [8, 1024], P('dp'), may hold values from 0 to 7, never falling along the last dimension, each value on 1 to 256 neighbouring positions
- norm1_gain: bfloat16 [1024], P('dp'), may hold values from 0.25 to 1.75
- q_weight: bfloat16 [1024, 2048], P('dp', 'tensor'), may hold values from -0.1875 to 0.1875
- key_projection: bfloat16 [1024, 1024], P('dp', 'tensor'), may hold values from -0.1875 to 0.1875
- value_projection: bfloat16 [1024, 1024], P('dp', 'tensor'), may hold values from -0.1875 to 0.1875
- q_gain: bfloat16 [128], P('dp'), may hold values from 0.25 to 1.75
- k_gain: bfloat16 [128], P('dp'), may hold values from 0.25 to 1.75
- o_weight: bfloat16 [2048, 1024], P('tensor', 'dp'), may hold values from -2 to 2
- norm2_gain: bfloat16 [1024], P('dp'), may hold values from 0.25 to 1.75
- gate_weight: bfloat16 [1024, 3072], P('dp', 'tensor'), may hold values from -0.1875 to 0.1875
- up_weight: bfloat16 [1024, 3072], P('dp', 'tensor'), may hold values from -0.1875 to 0.1875
- down_weight: bfloat16 [3072, 1024], P('tensor', 'dp'), may hold values from -0.109375 to 0.109375
- out_grad: bfloat16 [8192, 1024], P(('dp', 'tensor')), may hold values from -6 to 6
Outputs:
- layer_out: bfloat16 [8192, 1024], P(('dp', 'tensor'))
- tokens_grad: float32 [8192, 1024], P(('dp', 'tensor'))
- norm1_grad: float32 [1024], P('dp')
- q_weight_grad: float32 [1024, 2048], P('dp', 'tensor')
- k_weight_grad: float32 [1024, 1024], P('dp', 'tensor')
- v_weight_grad: float32 [1024, 1024], P('dp', 'tensor')
- q_gain_grad: float32 [128], P('dp')
- k_gain_grad: float32 [128], P('dp')
- o_weight_grad: float32 [2048, 1024], P('tensor', 'dp')
- norm2_grad: float32 [1024], P('dp')
- gate_weight_grad: float32 [1024, 3072], P('dp', 'tensor')
- up_weight_grad: float32 [1024, 3072], P('dp', 'tensor')
- down_weight_grad: float32 [3072, 1024], P('tensor', 'dp')
Inputs may be any that keep to these rules, and one draw needn't show every extreme that they name: `block_ids`: in each row block numbers never fall and every number from the least to the largest is used; each block has 1 to 256 tokens and some block has exactly 256.
All inputs are finite; a program needn't handle non-finite values.
Results may differ from a plain program's by a relative error of at most 0.017.
Values may be sent and summed in bfloat16 or wider, within the bound.
A program may use at most 128 MiB of HBM per device.

v0:
```python
from functools import partial
import jax
import jax.numpy as jnp
from jax import lax
from jax.sharding import PartitionSpec as P

EPSILON = 1e-06
BASE_FREQ = 1000000.0
MASKED = -1e30


def rms_scale(values, gain):
    return values * lax.rsqrt(jnp.mean(values * values, axis=-1, keepdims=True) + EPSILON) * gain


def rotate(values, cosine, sine):
    half = values.shape[-1] // 2
    turned = jnp.concatenate([-values[..., half:], values[..., :half]], axis=-1)
    return values * cosine + turned * sine


def angles(sequence_length, width):
    half = width // 2
    inverse = BASE_FREQ ** (-2.0 * jnp.arange(half, dtype=jnp.float32) / width)
    places = jnp.arange(sequence_length, dtype=jnp.float32)
    turns = places[:, None] * inverse[None, :]
    turns = jnp.concatenate([turns, turns], axis=-1)
    return (jnp.cos(turns)[:, None, :], jnp.sin(turns)[:, None, :])


def shape_heads(raw, gain, cosine, sine):
    return rotate(rms_scale(raw, gain), cosine, sine)


def contract_rows(left, right):
    return lax.dot_general(
        left, right, (((0,), (0,)), ((), ())), preferred_element_type=jnp.float32
    )


def contract_cols(left, right):
    return lax.dot_general(
        left, right, (((1,), (1,)), ((), ())), preferred_element_type=jnp.float32
    )


def attend_forward(queries_rot, keys_rot, rotated_values, block_of):
    sequence_length, heads, width = queries_rot.shape
    kv_heads = keys_rot.shape[1]
    head_group = heads // kv_heads
    extent_size = min(512, sequence_length)
    count = sequence_length // extent_size
    scale = width ** (-0.5)

    def one_block(inputs):
        query_block_index, block_rows = inputs
        grouped_heads = query_block_index.reshape(extent_size, kv_heads, head_group, width)
        scores = (
            jnp.einsum(
                "qhgd,khd->hgqk", grouped_heads, keys_rot, preferred_element_type=jnp.float32
            )
            * scale
        )
        seen = block_of[None, :] <= block_rows[:, None]
        scores = jnp.where(seen, scores, MASKED)
        highest = jnp.max(scores, axis=-1, keepdims=True)
        raised = jnp.exp(scores - highest)
        totals = jnp.sum(raised, axis=-1, keepdims=True)
        weights = (raised / totals).astype(jnp.bfloat16)
        mixed = jnp.einsum(
            "hgqk,khd->qhgd", weights, rotated_values, preferred_element_type=jnp.float32
        )
        return (
            mixed.reshape(extent_size, heads * width),
            highest[..., 0] + jnp.log(totals[..., 0]),
        )

    mixed, log_totals = lax.map(
        one_block,
        (
            queries_rot.reshape(count, extent_size, heads, width),
            block_of.reshape(count, extent_size),
        ),
    )
    return (mixed.reshape(sequence_length, heads * width), log_totals)


def attend_backward(queries_rot, keys_rot, rotated_values, block_of, log_totals, mixed_grad):
    sequence_length, heads, width = queries_rot.shape
    kv_heads = keys_rot.shape[1]
    head_group = heads // kv_heads
    extent_size = min(512, sequence_length)
    count = sequence_length // extent_size
    scale = width ** (-0.5)

    def one_block(carry, inputs):
        key_acc, value_acc = carry
        query_block_index, block_rows, log_block, grad_block = inputs
        grouped_heads = query_block_index.reshape(extent_size, kv_heads, head_group, width)
        grad_grouped = grad_block.reshape(extent_size, kv_heads, head_group, width)
        scores = (
            jnp.einsum(
                "qhgd,khd->hgqk", grouped_heads, keys_rot, preferred_element_type=jnp.float32
            )
            * scale
        )
        seen = block_of[None, :] <= block_rows[:, None]
        scores = jnp.where(seen, scores, MASKED)
        weights = jnp.exp(scores - log_block[..., None])
        weight_grad = jnp.einsum(
            "qhgd,khd->hgqk", grad_grouped, rotated_values, preferred_element_type=jnp.float32
        )
        centre = jnp.sum(weights * weight_grad, axis=-1, keepdims=True)
        score_grad = (weights * (weight_grad - centre)).astype(jnp.bfloat16)
        query_grad = (
            jnp.einsum("hgqk,khd->qhgd", score_grad, keys_rot, preferred_element_type=jnp.float32)
            * scale
        )
        key_acc = (
            key_acc
            + jnp.einsum(
                "hgqk,qhgd->khd", score_grad, grouped_heads, preferred_element_type=jnp.float32
            )
            * scale
        )
        value_acc = value_acc + jnp.einsum(
            "hgqk,qhgd->khd",
            weights.astype(jnp.bfloat16),
            grad_grouped,
            preferred_element_type=jnp.float32,
        )
        return ((key_acc, value_acc), query_grad.reshape(extent_size, heads * width))

    zeros = jnp.zeros((sequence_length, kv_heads, width), jnp.float32)
    (key_grad, value_grad), query_grad = lax.scan(
        one_block,
        (zeros, zeros),
        (
            queries_rot.reshape(count, extent_size, heads, width),
            block_of.reshape(count, extent_size),
            log_totals,
            mixed_grad.reshape(count, extent_size, heads, width),
        ),
    )
    return (query_grad.reshape(sequence_length, heads, width), key_grad, value_grad)


def body(
    tokens,
    block_ids,
    norm1_gain,
    q_weight,
    key_projection,
    value_projection,
    q_gain,
    k_gain,
    o_weight,
    norm2_gain,
    gate_weight,
    up_weight,
    down_weight,
    out_grad,
):
    shards = (
        norm1_gain,
        q_weight,
        key_projection,
        value_projection,
        q_gain,
        k_gain,
        o_weight,
        norm2_gain,
        gate_weight,
        up_weight,
        down_weight,
    )
    gathered = (
        lax.all_gather(shards[0], "dp", axis=0, tiled=True),
        lax.all_gather(shards[1], "dp", axis=0, tiled=True),
        lax.all_gather(shards[2], "dp", axis=0, tiled=True),
        lax.all_gather(shards[3], "dp", axis=0, tiled=True),
        lax.all_gather(shards[4], "dp", axis=0, tiled=True),
        lax.all_gather(shards[5], "dp", axis=0, tiled=True),
        lax.all_gather(shards[6], "dp", axis=1, tiled=True),
        lax.all_gather(shards[7], "dp", axis=0, tiled=True),
        lax.all_gather(shards[8], "dp", axis=0, tiled=True),
        lax.all_gather(shards[9], "dp", axis=0, tiled=True),
        lax.all_gather(shards[10], "dp", axis=1, tiled=True),
    )
    (
        gain_first,
        q_mat,
        key_matrix,
        value_matrix,
        q_scale,
        k_scale,
        o_mat,
        gain_second,
        gate_mat,
        up_mat,
        down_mat,
    ) = gathered
    block_of = block_ids[0]
    sequence_length = block_of.shape[0]
    head_dim = q_scale.shape[0]
    q_cols = q_weight.shape[1]
    kv_cols = key_projection.shape[1]
    ff_local = gate_weight.shape[1]
    heads = q_cols // head_dim
    kv_heads = kv_cols // head_dim
    cosine, sine = angles(sequence_length, head_dim)
    acts = tokens.astype(jnp.float32)
    first_gain = gain_first.astype(jnp.float32)
    second_gain = gain_second.astype(jnp.float32)
    qkv_mat = jnp.concatenate([q_mat, key_matrix, value_matrix], axis=1)
    gate_up = jnp.concatenate([gate_mat, up_mat], axis=1)
    normed_own = rms_scale(acts, first_gain).astype(jnp.bfloat16)
    piece = lax.all_gather(normed_own, "tensor", axis=0, tiled=True)
    projected = jnp.dot(piece, qkv_mat, preferred_element_type=jnp.float32)
    normalized_input = piece
    q_raw = projected[:, :q_cols].reshape(sequence_length, heads, head_dim)
    key_unrotated = projected[:, q_cols : q_cols + kv_cols].reshape(
        sequence_length, kv_heads, head_dim
    )
    rotated_values = (
        projected[:, q_cols + kv_cols :]
        .astype(jnp.bfloat16)
        .reshape(sequence_length, kv_heads, head_dim)
    )
    head_shaper = partial(shape_heads, cosine=cosine, sine=sine)
    q_shaped, q_pull = jax.vjp(head_shaper, q_raw, q_scale.astype(jnp.float32))
    k_shaped, k_pull = jax.vjp(head_shaper, key_unrotated, k_scale.astype(jnp.float32))
    queries_rot = q_shaped.astype(jnp.bfloat16)
    keys_rot = k_shaped.astype(jnp.bfloat16)
    mixed_full, log_totals = attend_forward(queries_rot, keys_rot, rotated_values, block_of)
    mixed = mixed_full.astype(jnp.bfloat16)
    state = acts + lax.psum_scatter(
        jnp.dot(mixed, o_mat, preferred_element_type=jnp.float32),
        "tensor",
        scatter_dimension=0,
        tiled=True,
    )
    normed_two_own = rms_scale(state, second_gain).astype(jnp.bfloat16)
    piece = lax.all_gather(normed_two_own, "tensor", axis=0, tiled=True)
    gate_both = jnp.dot(piece, gate_up, preferred_element_type=jnp.float32)
    normed_two = piece
    gate_pre = gate_both[:, :ff_local]
    up_pre = gate_both[:, ff_local:]
    sigmoid_gate = jax.nn.sigmoid(gate_pre)
    silu_gate = gate_pre * sigmoid_gate
    inner = (silu_gate * up_pre).astype(jnp.bfloat16)
    layer_sum = state + lax.psum_scatter(
        jnp.dot(inner, down_mat, preferred_element_type=jnp.float32).astype(jnp.bfloat16),
        "tensor",
        scatter_dimension=0,
        tiled=True,
    ).astype(jnp.float32)
    layer_out = layer_sum.astype(jnp.bfloat16)
    gathered = (
        lax.all_gather(shards[0], "dp", axis=0, tiled=True),
        lax.all_gather(shards[1], "dp", axis=0, tiled=True),
        lax.all_gather(shards[2], "dp", axis=0, tiled=True),
        lax.all_gather(shards[3], "dp", axis=0, tiled=True),
        lax.all_gather(shards[4], "dp", axis=0, tiled=True),
        lax.all_gather(shards[5], "dp", axis=0, tiled=True),
        lax.all_gather(shards[6], "dp", axis=1, tiled=True),
        lax.all_gather(shards[7], "dp", axis=0, tiled=True),
        lax.all_gather(shards[8], "dp", axis=0, tiled=True),
        lax.all_gather(shards[9], "dp", axis=0, tiled=True),
        lax.all_gather(shards[10], "dp", axis=1, tiled=True),
    )
    (
        gain_first,
        q_mat,
        key_matrix,
        value_matrix,
        q_scale,
        k_scale,
        o_mat,
        gain_second,
        gate_mat,
        up_mat,
        down_mat,
    ) = gathered
    qkv_mat = jnp.concatenate([q_mat, key_matrix, value_matrix], axis=1)
    gate_up = jnp.concatenate([gate_mat, up_mat], axis=1)
    piece = lax.all_gather(out_grad, "tensor", axis=0, tiled=True)
    inner_grad = contract_cols(piece, down_mat)
    grad_full = piece
    down_grad = contract_rows(inner, grad_full)
    gate_grad = inner_grad * up_pre * sigmoid_gate * (1.0 + gate_pre * (1.0 - sigmoid_gate))
    up_grad = inner_grad * silu_gate
    gate_up_grad = jnp.concatenate([gate_grad, up_grad], axis=1).astype(jnp.bfloat16)
    gate_up_wgrad = contract_rows(normed_two, gate_up_grad)
    normed_two_grad = lax.psum_scatter(
        contract_cols(gate_up_grad, gate_up).astype(jnp.bfloat16),
        "tensor",
        scatter_dimension=0,
        tiled=True,
    ).astype(jnp.float32)
    second_pull = jax.vjp(rms_scale, state, second_gain)[1]
    state_back, second_part = second_pull(normed_two_grad)
    state_grad = out_grad.astype(jnp.float32) + state_back
    piece = lax.all_gather(state_grad.astype(jnp.bfloat16), "tensor", axis=0, tiled=True)
    mixed_grad = contract_cols(piece, o_mat)
    o_grad = contract_rows(mixed, piece)
    q_rot_grad, k_rot_grad, v_grad = attend_backward(
        queries_rot, keys_rot, rotated_values, block_of, log_totals, mixed_grad.astype(jnp.bfloat16)
    )
    q_raw_grad, q_part = q_pull(q_rot_grad)
    k_raw_grad, k_part = k_pull(k_rot_grad)
    qkv_grad = jnp.concatenate(
        [
            q_raw_grad.reshape(sequence_length, q_cols),
            k_raw_grad.reshape(sequence_length, kv_cols),
            v_grad.reshape(sequence_length, kv_cols),
        ],
        axis=1,
    ).astype(jnp.bfloat16)
    qkv_wgrad = contract_rows(normalized_input, qkv_grad)
    normed_grad = lax.psum_scatter(
        contract_cols(qkv_grad, qkv_mat).astype(jnp.bfloat16),
        "tensor",
        scatter_dimension=0,
        tiled=True,
    ).astype(jnp.float32)
    first_pull = jax.vjp(rms_scale, acts, first_gain)[1]
    acts_back, first_part = first_pull(normed_grad)
    tokens_grad = state_grad + acts_back
    q_wgrad = qkv_wgrad[:, :q_cols]
    k_wgrad = qkv_wgrad[:, q_cols : q_cols + kv_cols]
    v_wgrad = qkv_wgrad[:, q_cols + kv_cols :]
    (
        first_sum,
        q_sum,
        k_sum,
        v_sum,
        qs_sum,
        ks_sum,
        o_sum,
        second_sum,
        gate_sum,
        up_sum,
        down_sum,
    ) = (
        lax.psum_scatter(first_part, "dp", scatter_dimension=0, tiled=True),
        lax.psum_scatter(q_wgrad, "dp", scatter_dimension=0, tiled=True),
        lax.psum_scatter(k_wgrad, "dp", scatter_dimension=0, tiled=True),
        lax.psum_scatter(v_wgrad, "dp", scatter_dimension=0, tiled=True),
        lax.psum_scatter(q_part, "dp", scatter_dimension=0, tiled=True),
        lax.psum_scatter(k_part, "dp", scatter_dimension=0, tiled=True),
        lax.psum_scatter(o_grad, "dp", scatter_dimension=1, tiled=True),
        lax.psum_scatter(second_part, "dp", scatter_dimension=0, tiled=True),
        lax.psum_scatter(gate_up_wgrad[:, :ff_local], "dp", scatter_dimension=0, tiled=True),
        lax.psum_scatter(gate_up_wgrad[:, ff_local:], "dp", scatter_dimension=0, tiled=True),
        lax.psum_scatter(down_grad, "dp", scatter_dimension=1, tiled=True),
    )
    first_total, second_total, qs_total, ks_total = lax.psum(
        (first_sum, second_sum, qs_sum, ks_sum), "tensor"
    )
    return (
        layer_out,
        tokens_grad,
        first_total,
        q_sum,
        k_sum,
        v_sum,
        qs_total,
        ks_total,
        o_sum,
        second_total,
        gate_sum,
        up_sum,
        down_sum,
    )


def solution(mesh):
    return jax.shard_map(
        body,
        mesh=mesh,
        in_specs=(
            P(("dp", "tensor"), None),
            P("dp", None),
            P("dp"),
            P("dp", "tensor"),
            P("dp", "tensor"),
            P("dp", "tensor"),
            P("dp"),
            P("dp"),
            P("tensor", "dp"),
            P("dp"),
            P("dp", "tensor"),
            P("dp", "tensor"),
            P("tensor", "dp"),
            P(("dp", "tensor"), None),
        ),
        out_specs=(
            P(("dp", "tensor"), None),
            P(("dp", "tensor"), None),
            P("dp"),
            P("dp", "tensor"),
            P("dp", "tensor"),
            P("dp", "tensor"),
            P("dp"),
            P("dp"),
            P("tensor", "dp"),
            P("dp"),
            P("dp", "tensor"),
            P("dp", "tensor"),
            P("tensor", "dp"),
        ),
        check_vma=False,
    )
```

profile of v0, /device:TPU:0, one launch (start us, length us, event | category | flops | bytes accessed | tf_op | source)
XLA Modules:
  0.0 1014.9 jit_solution(3832472821615925314)
XLA Ops:
  8.0 10.4 %all-gather = bf16[8,1,128]{2,1,0:T(2,128)(2,1)S(1)} all-gather(bf16[1,1,128]{2,1,0:T(2,128)(2,1)} %bitcast.258), channel_id=1, replica_groups=mesh['dp'=8,'tensor'=4] {'dp'}, dimensions={0}, use_global_device_ids=true | all-gather | bytes 2304 | tf_op jit(solution)/shard_map/all_gather | solution.py:178
  43.1 13.8 %all-reduce.12 = (bf16[128]{0:T(256)(128)(2,1)S(1)}, bf16[128]{0:T(256)(128)(2,1)S(1)}) all-reduce(bf16[128]{0:T(256)(128)(2,1)S(1)} %dynamic-update-slice, bf16[128]{0:T(256)(128)(2,1)S(1)} %dynamic-update-slice.1), channel_id=1, replica_groups=mesh['dp'=8,'tensor'=4] {'dp'}, use_global_device_ids=true, to_apply=%add.4 | all-reduce | flops 256 | bytes 1024
  112.9 20.0 %while.27 = (s32[]{:T(128)}, bf16[2,512,512]{2,1,0:T(8,128)(2,1)}, f32[2,2,2,512]{3,2,1,0:T(2,128)S(1)}, s32[1,1024]{1,0:T(1,128)S(1)}, s32[2,512]{1,0:T(2,128)S...) while((s32[]{:T(128)}, bf16[2,512,512]{2,1,0:T(8,128)(2,1)}, ...), condition=%wide.region_6.7_spmd, body=%wide.region_3.6_spmd.sunk | while | flops 1099429888 | bytes 32582248 | solution.py:78
  148.0 65.8 %reduce-scatter.12.cloned.1.call-done = f32[256,1024]{1,0:T(8,128)} async-done(((f32[1024,1024]{1,0:T(8,128)}), f32[256,1024]{1,0:T(8,128)}) %reduce-scatter.12.cloned.1.call-update) | async-done | bytes 1048592 | tf_op jit(solution)/shard_map/reduce_scatter | solution.py:237
  217.9 23.7 %all-gather.20.cloned.1.call-done = bf16[1024,768]{1,0:T(8,128)(2,1)} async-done(((bf16[128,768]{1,0:T(8,128)(2,1)}), bf16[1024,768]{1,0:T(8,128)(2,1)}) %all-gather.20.cloned.1.call-update) | async-done | bytes 1572880 | tf_op jit(solution)/shard_map/all_gather | solution.py:186
  244.4 24.6 %all-gather.22.cloned.1.call-done = bf16[1024,768]{1,0:T(8,128)(2,1)} async-done(((bf16[128,768]{1,0:T(8,128)(2,1)}), bf16[1024,768]{1,0:T(8,128)(2,1)}) %all-gather.22.cloned.1.call-update) | async-done | bytes 1572880 | tf_op jit(solution)/shard_map/all_gather | solution.py:187
  271.7 45.1 %all-gather.18.cloned.1.call-done = bf16[1024,1024]{1,0:T(8,128)(2,1)} async-done(((bf16[256,1024]{1,0:T(8,128)(2,1)}), bf16[1024,1024]{1,0:T(8,128)(2,1)}) %all-gather.18.cloned.1.call-update) | async-done | bytes 2097168 | tf_op jit(solution)/shard_map/all_gather | solution.py:244
  325.4 17.9 %all-gather.24.cloned.1.call-done = bf16[768,1024]{1,0:T(8,128)(2,1)} async-done(((bf16[768,128]{1,0:T(8,128)(2,1)}), bf16[768,1024]{1,0:T(8,128)(2,1)}) %all-gather.24.cloned.1.call-update) | async-done | bytes 1572880 | tf_op jit(solution)/shard_map/all_gather | solution.py:188
  343.3 47.3 %all-gather.26.cloned.1.call-done = bf16[1024,1024]{1,0:T(8,128)(2,1)} async-done(((bf16[256,1024]{1,0:T(8,128)(2,1)}), bf16[1024,1024]{1,0:T(8,128)(2,1)}) %all-gather.26.cloned.1.call-update) | async-done | bytes 2097168 | tf_op jit(solution)/shard_map/all_gather | solution.py:287
  405.4 42.1 %reduce-scatter.16.cloned.1.call-done = bf16[256,1024]{1,0:T(8,128)(2,1)} async-done(((bf16[1024,1024]{1,0:T(8,128)(2,1)}), bf16[256,1024]{1,0:T(8,128)(2,1)}) %reduce-scatter.16.cloned.1.call-update) | async-done | bytes 524304 | tf_op jit(solution)/shard_map/reduce_scatter | solution.py:295
  453.1 43.6 %all-gather.28.cloned.1.call-done = bf16[1024,1024]{1,0:T(8,128)(2,1)} async-done(((bf16[256,1024]{1,0:T(8,128)(2,1)}), bf16[1024,1024]{1,0:T(8,128)(2,1)}) %all-gather.28.cloned.1.call-update) | async-done | bytes 2097168 | tf_op jit(solution)/shard_map/all_gather | solution.py:304
  501.0 81.2 %while.28 = (s32[]{:T(128)}, f32[1024,2,128]{0,2,1:T(8,128)S(1)}, f32[1024,2,128]{0,2,1:T(8,128)}, f32[2,512,512]{1,0,2:T(2,128)}, bf16[2,512,4,128]{3,1,2,0:T(8...) while((s32[]{:T(128)}, f32[1024,2,128]{0,2,1:T(8,128)S(1)}, ...), condition=%wide.region_14.15_spmd.clone, body=%wide.region_12.14_spmd.clone.sunk | while | flops 2717906944 | bytes 181995984 | solution.py:135
  513.2 19.5 %dynamic_update_slice.19 = f32[2,512,512]{1,0,2:T(2,128)} dynamic-update-slice(f32[2,512,512]{1,0,2:T(2,128)} %get-tuple-element.505, f32[1,512,512]{1,0,2:T(1,128)S(1)} %copy.162, s32[]{:T(128)} %get-tuple-element.502, s32[]{:T(128)} %constant.43.clone.1..sunk, s32[]{:T(128)} %constant.43.clone.1..sunk) | dynamic-update-slice | bytes 2097156 | tf_op jit(solution)/shard_map/while/body/jit(dynamic_update_index_in_dim)/dynamic_update_slice | solution.py:78
  553.3 19.5 %dynamic_update_slice.19 = f32[2,512,512]{1,0,2:T(2,128)} dynamic-update-slice(f32[2,512,512]{1,0,2:T(2,128)} %get-tuple-element.505, f32[1,512,512]{1,0,2:T(1,128)S(1)} %copy.162, s32[]{:T(128)} %get-tuple-element.502, s32[]{:T(128)} %constant.43.clone.1..sunk, s32[]{:T(128)} %constant.43.clone.1..sunk) | dynamic-update-slice | bytes 2097156 | tf_op jit(solution)/shard_map/while/body/jit(dynamic_update_index_in_dim)/dynamic_update_slice | solution.py:78
  646.0 14.1 %all-reduce.10 = (f32[1024]{0:T(1024)S(1)}, f32[128]{0:T(128)S(1)}, f32[128]{0:T(128)S(1)}, f32[1024]{0:T(1024)S(1)}) all-reduce(f32[1024]{0:T(1024)S(1)} %get-tuple-element.257, f32[128]{0:T(128)S(1)} %get-tuple-element.251, f32[128]{0:T(128)S(1)} %get-tuple-element.255, ...), channel_id=6, replica_groups=mesh['dp'=8,'tensor'=4] {'dp'}, use_global_device_ids=true, to_apply=%region_20.21.clone | all-reduce | flops 2304 | bytes 18432
  660.4 11.4 %all-reduce.11 = (f32[128]{0:T(128)}, f32[16]{0:T(128)}, f32[16]{0:T(128)}, f32[128]{0:T(128)}) all-reduce(f32[128]{0:T(128)S(1)} %dynamic-slice.3, f32[16]{0:T(128)S(1)} %dynamic-slice.5, f32[16]{0:T(128)S(1)} %dynamic-slice.7, f32[128]{0:T(128)S(1)} %dynamic-slice.9), channel_id=1, replica_groups=mesh['dp'=8,'tensor'=4] {'tensor'}, use_global_device_ids=true, to_apply=%region_21.22 | all-reduce | flops 288 | bytes 2304 | tf_op jit(solution)/shard_map/psum | solution.py:358
  671.8 18.0 %reduce-scatter.14.cloned.1.call-done = bf16[256,1024]{1,0:T(8,128)(2,1)} async-done(((bf16[1024,1024]{1,0:T(8,128)(2,1)}), bf16[256,1024]{1,0:T(8,128)(2,1)}) %reduce-scatter.14.cloned.1.call-update) | async-done | bytes 524304 | tf_op jit(solution)/shard_map/reduce_scatter | solution.py:252
  692.8 46.2 %reduce-scatter.28.cloned.1.call-done = f32[128,768]{1,0:T(8,128)} async-done(((f32[1024,768]{1,0:T(8,128)}), f32[128,768]{1,0:T(8,128)}) %reduce-scatter.28.cloned.1.call-update) | async-done | bytes 393232 | tf_op jit(solution)/shard_map/reduce_scatter | solution.py:354
  739.0 49.9 %reduce-scatter.30.cloned.1.call-done = f32[128,768]{1,0:T(8,128)} async-done(((f32[1024,768]{1,0:T(8,128)}), f32[128,768]{1,0:T(8,128)}) %reduce-scatter.30.cloned.1.call-update) | async-done | bytes 393232 | tf_op jit(solution)/shard_map/reduce_scatter | solution.py:355
  788.9 49.9 %reduce-scatter.32.cloned.1.call-done = f32[768,128]{1,0:T(8,128)} async-done(((f32[768,1024]{1,0:T(8,128)}), f32[768,128]{1,0:T(8,128)}) %reduce-scatter.32.cloned.1.call-update) | async-done | bytes 393232 | tf_op jit(solution)/shard_map/reduce_scatter | solution.py:356
  838.8 39.6 %reduce-scatter.22.cloned.1.call-done = f32[128,256]{1,0:T(8,128)} async-done(((f32[1024,256]{1,0:T(8,128)}), f32[128,256]{1,0:T(8,128)}) %reduce-scatter.22.cloned.1.call-update) | async-done | bytes 131088 | tf_op jit(solution)/shard_map/reduce_scatter | solution.py:348
  878.4 39.6 %reduce-scatter.24.cloned.1.call-done = f32[128,256]{1,0:T(8,128)} async-done(((f32[1024,256]{1,0:T(8,128)}), f32[128,256]{1,0:T(8,128)}) %reduce-scatter.24.cloned.1.call-update) | async-done | bytes 131088 | tf_op jit(solution)/shard_map/reduce_scatter | solution.py:349
  918.0 45.0 %reduce-scatter.26.cloned.1.call-done = f32[512,128]{1,0:T(8,128)} async-done(((f32[512,1024]{1,0:T(8,128)}), f32[512,128]{1,0:T(8,128)}) %reduce-scatter.26.cloned.1.call-update) | async-done | bytes 262160 | tf_op jit(solution)/shard_map/reduce_scatter | solution.py:352
  963.0 44.9 %reduce-scatter.20.cloned.1.call-done = f32[128,512]{1,0:T(8,128)} async-done(((f32[1024,512]{1,0:T(8,128)}), f32[128,512]{1,0:T(8,128)}) %reduce-scatter.20.cloned.1.call-update) | async-done | bytes 262160 | tf_op jit(solution)/shard_map/reduce_scatter | solution.py:347
  (354 shorter events, 264.8 us)
Async XLA Ops:
  7.2 62.8 %all-gather.14.cloned.1.call-start = ((), (), s32[]{:S(2)}) async-start(), calls=%async_computation.12 | async-start | bytes 1179648 | tf_op jit(solution)/shard_map/all_gather | solution.py:179
  8.0 75.9 %all-gather.12.cloned.1.call-start = ((), (), s32[]{:S(2)}) async-start(), calls=%async_computation.11 | async-start | bytes 2621440 | tf_op jit(solution)/shard_map/all_gather | solution.py:218
  21.7 111.1 %all-gather.16.cloned.1.call-start = ((), (), s32[]{:S(2)}) async-start(), calls=%async_computation.13 | async-start | bytes 1179648 | tf_op jit(solution)/shard_map/all_gather | solution.py:184
  22.5 191.3 %reduce-scatter.12.cloned.1.call-start = ((), (), s32[]{:S(2)}) async-start(), calls=%async_computation.14 | async-start | bytes 5242880 | tf_op jit(solution)/shard_map/reduce_scatter | solution.py:237
  138.0 75.8 %copy-start.17 = (bf16[256,1024]{1,0:T(8,128)(2,1)S(1)}, bf16[256,1024]{1,0:T(8,128)(2,1)}, u32[]{:S(2)}) copy-start(bf16[256,1024]{1,0:T(8,128)(2,1)} %param.18) | copy-start | bytes 1572868
  138.0 103.6 %all-gather.20.cloned.1.call-start = ((), (), s32[]{:S(2)}) async-start(), calls=%async_computation.16 | async-start | bytes 1769472 | tf_op jit(solution)/shard_map/all_gather | solution.py:186
  138.6 130.4 %all-gather.22.cloned.1.call-start = ((), (), s32[]{:S(2)}) async-start(), calls=%async_computation.17 | async-start | bytes 1769472 | tf_op jit(solution)/shard_map/all_gather | solution.py:187
  139.2 177.6 %all-gather.18.cloned.1.call-start = ((), (), s32[]{:S(2)}) async-start(), calls=%async_computation.15 | async-start | bytes 2621440 | tf_op jit(solution)/shard_map/all_gather | solution.py:244
  148.0 301.5 %copy-start.47 = (f32[8,1,128]{2,1,0:T(1,128)}, f32[8,1,128]{2,1,0:T(1,128)S(1)}, u32[]{:S(2)}) copy-start(f32[8,1,128]{2,1,0:T(1,128)S(1)} %convert_element_type.102) | copy-start | bytes 12292
  215.3 234.2 %copy-start.10 = (f32[256,1024]{1,0:T(8,128)}, f32[256,1024]{1,0:T(8,128)S(1)}, u32[]{:S(2)}) copy-start(f32[256,1024]{1,0:T(8,128)S(1)} %get-tuple-element.310) | copy-start | bytes 3145732
  215.3 234.2 %copy-start.55 = (f32[256]{0:T(256)}, f32[256]{0:T(256)S(1)}, u32[]{:S(2)}) copy-start(f32[256]{0:T(256)S(1)} %fusion.62) | copy-start | bytes 3076
  216.4 126.9 %all-gather.24.cloned.1.call-start = ((), (), s32[]{:S(2)}) async-start(), calls=%async_computation.18 | async-start | bytes 1769472 | tf_op jit(solution)/shard_map/all_gather | solution.py:188
  217.1 173.4 %all-gather.26.cloned.1.call-start = ((), (), s32[]{:S(2)}) async-start(), calls=%async_computation.20 | async-start | bytes 2621440 | tf_op jit(solution)/shard_map/all_gather | solution.py:287
  217.9 229.6 %reduce-scatter.16.cloned.1.call-start = ((), (), s32[]{:S(2)}) async-start(), calls=%async_computation.21 | async-start | bytes 2621440 | tf_op jit(solution)/shard_map/reduce_scatter | solution.py:295
  404.9 91.8 %all-gather.28.cloned.1.call-start = ((), (), s32[]{:S(2)}) async-start(), calls=%async_computation.22 | async-start | bytes 2621440 | tf_op jit(solution)/shard_map/all_gather | solution.py:304
  451.7 192.7 %reduce-scatter.18.cloned.1.call-start = ((), (), s32[]{:S(2)}) async-start(), calls=%async_computation.23 | async-start | bytes 2621440 | tf_op jit(solution)/shard_map/reduce_scatter | solution.py:321
  601.9 88.0 %reduce-scatter.14.cloned.1.call-start = ((), (), s32[]{:S(2)}) async-start(), calls=%async_computation.19 | async-start | bytes 2621440 | tf_op jit(solution)/shard_map/reduce_scatter | solution.py:252
  607.8 131.2 %reduce-scatter.28.cloned.1.call-start = ((), (), s32[]{:S(2)}) async-start(), calls=%async_computation.28 | async-start | bytes 3538944 | tf_op jit(solution)/shard_map/reduce_scatter | solution.py:354
  618.1 170.8 %reduce-scatter.30.cloned.1.call-start = ((), (), s32[]{:S(2)}) async-start(), calls=%async_computation.29 | async-start | bytes 3538944 | tf_op jit(solution)/shard_map/reduce_scatter | solution.py:355
  618.7 220.1 %reduce-scatter.32.cloned.1.call-start = ((), (), s32[]{:S(2)}) async-start(), calls=%async_computation.30 | async-start | bytes 3538944 | tf_op jit(solution)/shard_map/reduce_scatter | solution.py:356
  624.7 253.7 %reduce-scatter.22.cloned.1.call-start = ((), (), s32[]{:S(2)}) async-start(), calls=%async_computation.25 | async-start | bytes 1179648 | tf_op jit(solution)/shard_map/reduce_scatter | solution.py:348
  632.5 285.4 %reduce-scatter.24.cloned.1.call-start = ((), (), s32[]{:S(2)}) async-start(), calls=%async_computation.26 | async-start | bytes 1179648 | tf_op jit(solution)/shard_map/reduce_scatter | solution.py:349
  633.1 329.9 %reduce-scatter.26.cloned.1.call-start = ((), (), s32[]{:S(2)}) async-start(), calls=%async_computation.27 | async-start | bytes 2359296 | tf_op jit(solution)/shard_map/reduce_scatter | solution.py:352
  636.7 371.1 %reduce-scatter.20.cloned.1.call-start = ((), (), s32[]{:S(2)}) async-start(), calls=%async_computation.24 | async-start | bytes 2359296 | tf_op jit(solution)/shard_map/reduce_scatter | solution.py:347
  (82 other events, 900.1 us)
Sparse Core Ops, SparseCore 0:
  9.9 26.0 all-gather.13
  38.2 45.6 all-gather.11
  85.8 22.2 all-gather.15
  138.1 75.6 reduce-scatter.11
  215.5 26.0 all-gather.19
  243.4 25.5 all-gather.21
  271.1 45.6 all-gather.17
  318.7 24.5 all-gather.23
  344.9 45.6 all-gather.25
  405.1 42.3 reduce-scatter.15
  451.8 44.8 all-gather.27
  602.0 42.4 reduce-scatter.17
  646.7 43.0 reduce-scatter.13
  693.7 45.2 reduce-scatter.27
  742.8 46.0 reduce-scatter.29
  792.7 46.0 reduce-scatter.31
  842.4 35.9 reduce-scatter.21
  882.0 35.9 reduce-scatter.23
  921.8 41.1 reduce-scatter.25
  966.7 41.1 reduce-scatter.19
where the time goes:
time: 1020 us; the launch traced here: 1010 us
  waiting for transfers between devices  661 us (65%)
  local copies, waits for them, and re-layouts  105 us (10%)
  matrix products  100 us (10%)
  blocking collectives  77.2 us (8%)
  other arithmetic  52.2 us (5%)
  between operations  17.5 us (2%)
    reduce_scatter x1, waiting for transfers between devices, body(): lax.psum_scatter(jnp.dot(mixed, o_mat, preferred_element_type=jnp.float32...  65.8 us
    reduce_scatter x1, waiting for transfers between devices, body(): lax.psum_scatter(down_grad, 'dp', scatter_dimension=1, tiled=True)  49.9 us
    reduce_scatter x1, waiting for transfers between devices, body(): lax.psum_scatter(gate_up_wgrad[:, ff_local:], 'dp', scatter_dimension=0,...  49.9 us
    all_gather x1, waiting for transfers between devices, body(): piece = lax.all_gather(out_grad, 'tensor', axis=0, tiled=True)  47.3 us
    reduce_scatter x1, waiting for transfers between devices, body(): lax.psum_scatter(gate_up_wgrad[:, :ff_local], 'dp', scatter_dimension=0,...  46.2 us
    all_gather x1, waiting for transfers between devices, body(): piece = lax.all_gather(normed_two_own, 'tensor', axis=0, tiled=True)  45.1 us
    reduce_scatter x1, waiting for transfers between devices, body(): lax.psum_scatter(o_grad, 'dp', scatter_dimension=1, tiled=True)  45 us
    reduce_scatter x1, waiting for transfers between devices, body(): lax.psum_scatter(q_wgrad, 'dp', scatter_dimension=0, tiled=True)  44.9 us
  transfers between devices with their start and end apart: 20, of which 18 were waited for; matrix products, arithmetic and copies ran while one was open for 12% of the time, Pallas kernels for 0%

commit v1 on v0

--- a/solution.py
+++ b/solution.py
@@ -7,6 +7,18 @@
 EPSILON = 1e-06
 BASE_FREQ = 1000000.0
 MASKED = -1e30
+
+
+def collect(x, axis, dim):
+    ways, here = (lax.axis_size(axis), lax.axis_index(axis))
+    grown, reach = (x, 1)
+    while reach < ways:
+        theirs = lax.ppermute(grown, axis, [(d, d ^ reach) for d in range(ways)])
+        mine_first = jnp.concatenate([grown, theirs], axis=dim)
+        theirs_first = jnp.concatenate([theirs, grown], axis=dim)
+        grown = jnp.where(here & reach == 0, mine_first, theirs_first)
+        reach = 2 * reach
+    return grown
 
 
 def rms_scale(values, gain):
@@ -241,7 +253,7 @@
         tiled=True,
     )
     normed_two_own = rms_scale(state, second_gain).astype(jnp.bfloat16)
-    piece = lax.all_gather(normed_two_own, "tensor", axis=0, tiled=True)
+    piece = collect(normed_two_own, "tensor", 0)
     gate_both = jnp.dot(piece, gate_up, preferred_element_type=jnp.float32)
     normed_two = piece
     gate_pre = gate_both[:, :ff_local]

time: 1020 us -> 975 us (0.956)
  waiting for transfers between devices: 661 us -> 609 us
    all_gather x1 -> x0, waiting for transfers between devices: 45.1 us -> none  [body(): piece = lax.all_gather(normed_two_own, 'tensor', axis=0, tiled=True)]
    ppermute x0 -> x2, waiting for transfers between devices: none -> 18.7 us  [collect(): theirs = lax.ppermute(grown, axis, [(d, d ^ reach) for d in range(ways)])]
    all_gather x1, waiting for transfers between devices: 23.7 us -> 8.14 us  [body(): lax.all_gather(shards[8], 'dp', axis=0, tiled=True)]
    unnamed x144 -> x146, local copies, waits for them, and re-layouts: 22.5 us -> 22.1 us
  transfers between devices with their start and end apart: 20 -> 21, of which waited for: 18 -> 19; matrix products, arithmetic and copies ran while one was open for 12% -> 13% of each run, Pallas kernels for 0% -> 0%
where the time goes in v1:
time: 975 us; the launch traced here: 968 us
  waiting for transfers between devices  609 us (62%)
  local copies, waits for them, and re-layouts  104 us (11%)
  matrix products  102 us (10%)
  blocking collectives  77.1 us (8%)
  other arithmetic  52.7 us (5%)
  between operations  17.2 us (2%)
    reduce_scatter x1, waiting for transfers between devices, body(): lax.psum_scatter(jnp.dot(mixed, o_mat, preferred_element_type=jnp.float32...  64.3 us
    reduce_scatter x1, waiting for transfers between devices, body(): lax.psum_scatter(gate_up_wgrad[:, ff_local:], 'dp', scatter_dimension=0,...  49.9 us
    reduce_scatter x1, waiting for transfers between devices, body(): lax.psum_scatter(down_grad, 'dp', scatter_dimension=1, tiled=True)  49.9 us
    all_gather x1, waiting for transfers between devices, body(): piece = lax.all_gather(out_grad, 'tensor', axis=0, tiled=True)  47.3 us
    reduce_scatter x1, waiting for transfers between devices, body(): lax.psum_scatter(gate_up_wgrad[:, :ff_local], 'dp', scatter_dimension=0,...  46.3 us
    reduce_scatter x1, waiting for transfers between devices, body(): lax.psum_scatter(q_wgrad, 'dp', scatter_dimension=0, tiled=True)  45 us
    reduce_scatter x1, waiting for transfers between devices, body(): lax.psum_scatter(o_grad, 'dp', scatter_dimension=1, tiled=True)  44.8 us
    all_gather x1, waiting for transfers between devices, body(): lax.all_gather(state_grad.astype(jnp.bfloat16), 'tensor', axis=0, tiled=T...  43.6 us
  transfers between devices with their start and end apart: 21, of which 19 were waited for; matrix products, arithmetic and copies ran while one was open for 13% of the time, Pallas kernels for 0%

profile of v1, /device:TPU:0, one launch (start us, length us, event | category | flops | bytes accessed | tf_op | source)
XLA Modules:
  0.0 968.2 jit_solution(11750981052881513641)
XLA Ops:
  8.0 10.4 %all-gather = bf16[8,1,128]{2,1,0:T(2,128)(2,1)S(1)} all-gather(bf16[1,1,128]{2,1,0:T(2,128)(2,1)} %bitcast.256), channel_id=1, replica_groups=mesh['dp'=8,'tensor'=4] {'dp'}, dimensions={0}, use_global_device_ids=true | all-gather | bytes 2304 | tf_op jit(solution)/shard_map/all_gather | solution.py:190
  22.6 9.7 %all_gather.52 = bf16[1024,256]{1,0:T(8,128)(2,1)S(1)} all-gather(bf16[128,256]{1,0:T(8,128)(2,1)S(1)} %copy-done.51), channel_id=1, replica_groups=mesh['dp'=8,'tensor'=4] {'dp'}, dimensions={0}, use_global_device_ids=true | all-gather | bytes 589824 | tf_op jit(solution)/shard_map/all_gather | solution.py:192
  43.1 13.8 %all-reduce.12 = (bf16[128]{0:T(256)(128)(2,1)S(1)}, bf16[128]{0:T(256)(128)(2,1)S(1)}) all-reduce(bf16[128]{0:T(256)(128)(2,1)S(1)} %dynamic-update-slice, bf16[128]{0:T(256)(128)(2,1)S(1)} %dynamic-update-slice.1), channel_id=1, replica_groups=mesh['dp'=8,'tensor'=4] {'dp'}, use_global_device_ids=true, to_apply=%add.4 | all-reduce | flops 256 | bytes 1024
  74.1 9.8 %all-gather.11.cloned.1.call-done = bf16[1024,1024]{1,0:T(8,128)(2,1)} async-done(((bf16[256,1024]{1,0:T(8,128)(2,1)}), bf16[1024,1024]{1,0:T(8,128)(2,1)}) %all-gather.11.cloned.1.call-update) | async-done | bytes 2097168 | tf_op jit(solution)/shard_map/all_gather | solution.py:230
  112.9 20.0 %while.27 = (s32[]{:T(128)}, bf16[2,512,512]{2,1,0:T(8,128)(2,1)}, f32[2,2,2,512]{3,2,1,0:T(2,128)S(1)}, s32[1,1024]{1,0:T(1,128)S(1)}, s32[2,512]{1,0:T(2,128)S...) while((s32[]{:T(128)}, bf16[2,512,512]{2,1,0:T(8,128)(2,1)}, ...), condition=%wide.region_6.7_spmd, body=%wide.region_3.6_spmd.sunk | while | flops 1099429888 | bytes 32582248 | solution.py:90
  149.5 64.3 %reduce-scatter.12.cloned.1.call-done = f32[256,1024]{1,0:T(8,128)} async-done(((f32[1024,1024]{1,0:T(8,128)}), f32[256,1024]{1,0:T(8,128)}) %reduce-scatter.12.cloned.1.call-update) | async-done | bytes 1048592 | tf_op jit(solution)/shard_map/reduce_scatter | solution.py:249
  217.0 11.9 %collective-permute-done = bf16[256,1024]{1,0:T(8,128)(2,1)S(1)} collective-permute-done((bf16[256,1024]{1,0:T(8,128)(2,1)S(1)}, bf16[256,1024]{1,0:T(8,128)(2,1)S(1)}, u32[]{:S(2)}, u32[]{:S(2)}) %collective-permute-start) | collective-permute-done | bytes 524320 | tf_op jit(solution)/shard_map/ppermute | solution.py:16
  244.4 24.6 %all-gather.19.cloned.1.call-done = bf16[1024,768]{1,0:T(8,128)(2,1)} async-done(((bf16[128,768]{1,0:T(8,128)(2,1)}), bf16[1024,768]{1,0:T(8,128)(2,1)}) %all-gather.19.cloned.1.call-update) | async-done | bytes 1572880 | tf_op jit(solution)/shard_map/all_gather | solution.py:199
  296.7 47.3 %all-gather.23.cloned.1.call-done = bf16[1024,1024]{1,0:T(8,128)(2,1)} async-done(((bf16[256,1024]{1,0:T(8,128)(2,1)}), bf16[1024,1024]{1,0:T(8,128)(2,1)}) %all-gather.23.cloned.1.call-update) | async-done | bytes 2097168 | tf_op jit(solution)/shard_map/all_gather | solution.py:299
  358.7 42.5 %reduce-scatter.16.cloned.1.call-done = bf16[256,1024]{1,0:T(8,128)(2,1)} async-done(((bf16[1024,1024]{1,0:T(8,128)(2,1)}), bf16[256,1024]{1,0:T(8,128)(2,1)}) %reduce-scatter.16.cloned.1.call-update) | async-done | bytes 524304 | tf_op jit(solution)/shard_map/reduce_scatter | solution.py:307
  406.9 43.6 %all-gather.25.cloned.1.call-done = bf16[1024,1024]{1,0:T(8,128)(2,1)} async-done(((bf16[256,1024]{1,0:T(8,128)(2,1)}), bf16[1024,1024]{1,0:T(8,128)(2,1)}) %all-gather.25.cloned.1.call-update) | async-done | bytes 2097168 | tf_op jit(solution)/shard_map/all_gather | solution.py:316
  454.7 81.2 %while.28 = (s32[]{:T(128)}, f32[1024,2,128]{0,2,1:T(8,128)S(1)}, f32[1024,2,128]{0,2,1:T(8,128)}, f32[2,512,512]{1,0,2:T(2,128)}, bf16[2,512,4,128]{3,1,2,0:T(8...) while((s32[]{:T(128)}, f32[1024,2,128]{0,2,1:T(8,128)S(1)}, ...), condition=%wide.region_14.15_spmd.clone, body=%wide.region_12.14_spmd.clone.sunk | while | flops 2717906944 | bytes 181995984 | solution.py:147
  467.0 19.5 %dynamic_update_slice.19 = f32[2,512,512]{1,0,2:T(2,128)} dynamic-update-slice(f32[2,512,512]{1,0,2:T(2,128)} %get-tuple-element.505, f32[1,512,512]{1,0,2:T(1,128)S(1)} %copy.162, s32[]{:T(128)} %get-tuple-element.502, s32[]{:T(128)} %constant.44.clone.1..sunk, s32[]{:T(128)} %constant.44.clone.1..sunk) | dynamic-update-slice | bytes 2097156 | tf_op jit(solution)/shard_map/while/body/jit(dynamic_update_index_in_dim)/dynamic_update_slice | solution.py:90
  507.0 19.5 %dynamic_update_slice.19 = f32[2,512,512]{1,0,2:T(2,128)} dynamic-update-slice(f32[2,512,512]{1,0,2:T(2,128)} %get-tuple-element.505, f32[1,512,512]{1,0,2:T(1,128)S(1)} %copy.162, s32[]{:T(128)} %get-tuple-element.502, s32[]{:T(128)} %constant.44.clone.1..sunk, s32[]{:T(128)} %constant.44.clone.1..sunk) | dynamic-update-slice | bytes 2097156 | tf_op jit(solution)/shard_map/while/body/jit(dynamic_update_index_in_dim)/dynamic_update_slice | solution.py:90
  599.7 14.1 %all-reduce.10 = (f32[1024]{0:T(1024)S(1)}, f32[128]{0:T(128)S(1)}, f32[128]{0:T(128)S(1)}, f32[1024]{0:T(1024)S(1)}) all-reduce(f32[1024]{0:T(1024)S(1)} %get-tuple-element.257, f32[128]{0:T(128)S(1)} %get-tuple-element.251, f32[128]{0:T(128)S(1)} %get-tuple-element.255, ...), channel_id=6, replica_groups=mesh['dp'=8,'tensor'=4] {'dp'}, use_global_device_ids=true, to_apply=%region_20.21.clone | all-reduce | flops 2304 | bytes 18432
  614.1 11.3 %all-reduce.11 = (f32[128]{0:T(128)}, f32[16]{0:T(128)}, f32[16]{0:T(128)}, f32[128]{0:T(128)}) all-reduce(f32[128]{0:T(128)S(1)} %dynamic-slice.3, f32[16]{0:T(128)S(1)} %dynamic-slice.5, f32[16]{0:T(128)S(1)} %dynamic-slice.7, f32[128]{0:T(128)S(1)} %dynamic-slice.9), channel_id=1, replica_groups=mesh['dp'=8,'tensor'=4] {'tensor'}, use_global_device_ids=true, to_apply=%region_21.22 | all-reduce | flops 288 | bytes 2304 | tf_op jit(solution)/shard_map/psum | solution.py:370
  625.4 18.0 %reduce-scatter.14.cloned.1.call-done = bf16[256,1024]{1,0:T(8,128)(2,1)} async-done(((bf16[1024,1024]{1,0:T(8,128)(2,1)}), bf16[256,1024]{1,0:T(8,128)(2,1)}) %reduce-scatter.14.cloned.1.call-update) | async-done | bytes 524304 | tf_op jit(solution)/shard_map/reduce_scatter | solution.py:264
  646.3 46.3 %reduce-scatter.28.cloned.1.call-done = f32[128,768]{1,0:T(8,128)} async-done(((f32[1024,768]{1,0:T(8,128)}), f32[128,768]{1,0:T(8,128)}) %reduce-scatter.28.cloned.1.call-update) | async-done | bytes 393232 | tf_op jit(solution)/shard_map/reduce_scatter | solution.py:366
  692.6 49.9 %reduce-scatter.30.cloned.1.call-done = f32[128,768]{1,0:T(8,128)} async-done(((f32[1024,768]{1,0:T(8,128)}), f32[128,768]{1,0:T(8,128)}) %reduce-scatter.30.cloned.1.call-update) | async-done | bytes 393232 | tf_op jit(solution)/shard_map/reduce_scatter | solution.py:367
  742.5 49.9 %reduce-scatter.32.cloned.1.call-done = f32[768,128]{1,0:T(8,128)} async-done(((f32[768,1024]{1,0:T(8,128)}), f32[768,128]{1,0:T(8,128)}) %reduce-scatter.32.cloned.1.call-update) | async-done | bytes 393232 | tf_op jit(solution)/shard_map/reduce_scatter | solution.py:368
  792.4 39.6 %reduce-scatter.22.cloned.1.call-done = f32[128,256]{1,0:T(8,128)} async-done(((f32[1024,256]{1,0:T(8,128)}), f32[128,256]{1,0:T(8,128)}) %reduce-scatter.22.cloned.1.call-update) | async-done | bytes 131088 | tf_op jit(solution)/shard_map/reduce_scatter | solution.py:360
  832.1 39.6 %reduce-scatter.24.cloned.1.call-done = f32[128,256]{1,0:T(8,128)} async-done(((f32[1024,256]{1,0:T(8,128)}), f32[128,256]{1,0:T(8,128)}) %reduce-scatter.24.cloned.1.call-update) | async-done | bytes 131088 | tf_op jit(solution)/shard_map/reduce_scatter | solution.py:361
  871.7 44.8 %reduce-scatter.26.cloned.1.call-done = f32[512,128]{1,0:T(8,128)} async-done(((f32[512,1024]{1,0:T(8,128)}), f32[512,128]{1,0:T(8,128)}) %reduce-scatter.26.cloned.1.call-update) | async-done | bytes 262160 | tf_op jit(solution)/shard_map/reduce_scatter | solution.py:364
  916.5 45.0 %reduce-scatter.20.cloned.1.call-done = f32[128,512]{1,0:T(8,128)} async-done(((f32[1024,512]{1,0:T(8,128)}), f32[128,512]{1,0:T(8,128)}) %reduce-scatter.20.cloned.1.call-update) | async-done | bytes 262160 | tf_op jit(solution)/shard_map/reduce_scatter | solution.py:359
  (358 shorter events, 275.1 us)
Async XLA Ops:
  7.2 62.8 %all-gather.13.cloned.1.call-start = ((), (), s32[]{:S(2)}) async-start(), calls=%async_computation.12 | async-start | bytes 1179648 | tf_op jit(solution)/shard_map/all_gather | solution.py:191
  8.0 75.9 %all-gather.11.cloned.1.call-start = ((), (), s32[]{:S(2)}) async-start(), calls=%async_computation.11 | async-start | bytes 2621440 | tf_op jit(solution)/shard_map/all_gather | solution.py:230
  21.7 111.1 %all-gather.15.cloned.1.call-start = ((), (), s32[]{:S(2)}) async-start(), calls=%async_computation.13 | async-start | bytes 1179648 | tf_op jit(solution)/shard_map/all_gather | solution.py:196
  22.5 191.3 %reduce-scatter.12.cloned.1.call-start = ((), (), s32[]{:S(2)}) async-start(), calls=%async_computation.14 | async-start | bytes 5242880 | tf_op jit(solution)/shard_map/reduce_scatter | solution.py:249
  138.0 103.6 %all-gather.17.cloned.1.call-start = ((), (), s32[]{:S(2)}) async-start(), calls=%async_computation.15 | async-start | bytes 1769472 | tf_op jit(solution)/shard_map/all_gather | solution.py:198
  138.6 130.4 %all-gather.19.cloned.1.call-start = ((), (), s32[]{:S(2)}) async-start(), calls=%async_computation.16 | async-start | bytes 1769472 | tf_op jit(solution)/shard_map/all_gather | solution.py:199
  139.2 157.5 %all-gather.21.cloned.1.call-start = ((), (), s32[]{:S(2)}) async-start(), calls=%async_computation.17 | async-start | bytes 1769472 | tf_op jit(solution)/shard_map/all_gather | solution.py:200
  140.0 204.0 %all-gather.23.cloned.1.call-start = ((), (), s32[]{:S(2)}) async-start(), calls=%async_computation.19 | async-start | bytes 2621440 | tf_op jit(solution)/shard_map/all_gather | solution.py:299
  140.7 260.6 %reduce-scatter.16.cloned.1.call-start = ((), (), s32[]{:S(2)}) async-start(), calls=%async_computation.20 | async-start | bytes 2621440 | tf_op jit(solution)/shard_map/reduce_scatter | solution.py:307
  149.5 253.7 %copy-start.47 = (f32[8,1,128]{2,1,0:T(1,128)}, f32[8,1,128]{2,1,0:T(1,128)S(1)}, u32[]{:S(2)}) copy-start(f32[8,1,128]{2,1,0:T(1,128)S(1)} %convert_element_type.102) | copy-start | bytes 12292
  215.3 188.0 %copy-start.10 = (f32[256,1024]{1,0:T(8,128)}, f32[256,1024]{1,0:T(8,128)S(1)}, u32[]{:S(2)}) copy-start(f32[256,1024]{1,0:T(8,128)S(1)} %get-tuple-element.310) | copy-start | bytes 3145732
  215.3 188.0 %copy-start.55 = (f32[256]{0:T(256)}, f32[256]{0:T(256)S(1)}, u32[]{:S(2)}) copy-start(f32[256]{0:T(256)S(1)} %fusion.63) | copy-start | bytes 3076
  215.4 13.4 %collective-permute-start = (bf16[256,1024]{1,0:T(8,128)(2,1)S(1)}, bf16[256,1024]{1,0:T(8,128)(2,1)S(1)}, u32[]{:S(2)}, u32[]{:S(2)}) collective-permute-start(bf16[256,1024]{1,0:T(8,128)(2,1)S(1)} %multiply_convert_fusion.3), channel_id=1, source_target_pairs={{0,1},{1,0},{2,3},{3,2},{4,5},{5,4},{6,7},{7,6},{8,9},{9,8},{10,11... | collective-permute-start | bytes 1572872 | tf_op jit(solution)/shard_map/ppermute | solution.py:16
  230.3 48.2 %collective-permute-start.1 = (bf16[512,1024]{1,0:T(8,128)(2,1)}, bf16[512,1024]{1,0:T(8,128)(2,1)S(1)}, u32[]{:S(2)}, u32[]{:S(2)}) collective-permute-start(bf16[512,1024]{1,0:T(8,128)(2,1)} %maximum_select_fusion.1), channel_id=1, source_target_pairs={{0,2},{1,3},{2,0},{3,1},{4,6},{5,7},{6,4},{7,5},{8,10},{9,11},{10,... | collective-permute-start | bytes 3145736 | tf_op jit(solution)/shard_map/ppermute | solution.py:16
  358.7 91.8 %all-gather.25.cloned.1.call-start = ((), (), s32[]{:S(2)}) async-start(), calls=%async_computation.21 | async-start | bytes 2621440 | tf_op jit(solution)/shard_map/all_gather | solution.py:316
  405.5 192.7 %reduce-scatter.18.cloned.1.call-start = ((), (), s32[]{:S(2)}) async-start(), calls=%async_computation.22 | async-start | bytes 2621440 | tf_op jit(solution)/shard_map/reduce_scatter | solution.py:333
  555.5 87.8 %reduce-scatter.14.cloned.1.call-start = ((), (), s32[]{:S(2)}) async-start(), calls=%async_computation.18 | async-start | bytes 2621440 | tf_op jit(solution)/shard_map/reduce_scatter | solution.py:264
  561.5 131.1 %reduce-scatter.28.cloned.1.call-start = ((), (), s32[]{:S(2)}) async-start(), calls=%async_computation.27 | async-start | bytes 3538944 | tf_op jit(solution)/shard_map/reduce_scatter | solution.py:366
  572.1 170.4 %reduce-scatter.30.cloned.1.call-start = ((), (), s32[]{:S(2)}) async-start(), calls=%async_computation.28 | async-start | bytes 3538944 | tf_op jit(solution)/shard_map/reduce_scatter | solution.py:367
  572.7 219.7 %reduce-scatter.32.cloned.1.call-start = ((), (), s32[]{:S(2)}) async-start(), calls=%async_computation.29 | async-start | bytes 3538944 | tf_op jit(solution)/shard_map/reduce_scatter | solution.py:368
  578.7 253.3 %reduce-scatter.22.cloned.1.call-start = ((), (), s32[]{:S(2)}) async-start(), calls=%async_computation.24 | async-start | bytes 1179648 | tf_op jit(solution)/shard_map/reduce_scatter | solution.py:360
  586.5 285.1 %reduce-scatter.24.cloned.1.call-start = ((), (), s32[]{:S(2)}) async-start(), calls=%async_computation.25 | async-start | bytes 1179648 | tf_op jit(solution)/shard_map/reduce_scatter | solution.py:361
  587.1 329.4 %reduce-scatter.26.cloned.1.call-start = ((), (), s32[]{:S(2)}) async-start(), calls=%async_computation.26 | async-start | bytes 2359296 | tf_op jit(solution)/shard_map/reduce_scatter | solution.py:364
  590.8 370.7 %reduce-scatter.20.cloned.1.call-start = ((), (), s32[]{:S(2)}) async-start(), calls=%async_computation.23 | async-start | bytes 2359296 | tf_op jit(solution)/shard_map/reduce_scatter | solution.py:359
  (84 other events, 981.0 us)
Sparse Core Ops, SparseCore 0:
  9.9 26.0 all-gather.12
  38.2 45.6 all-gather.10
  85.8 22.2 all-gather.14
  138.2 75.6 reduce-scatter.11
  215.5 26.0 all-gather.16
  243.4 25.5 all-gather.18
  270.9 25.7 all-gather.20
  298.3 45.6 all-gather.22
  358.8 42.4 reduce-scatter.15
  405.6 44.8 all-gather.24
  555.7 42.4 reduce-scatter.17
  600.3 43.0 reduce-scatter.13
  647.3 45.2 reduce-scatter.27
  696.4 46.0 reduce-scatter.29
  746.3 46.0 reduce-scatter.31
  796.0 35.9 reduce-scatter.21
  835.7 35.9 reduce-scatter.23
  875.4 41.0 reduce-scatter.25
  920.4 41.0 reduce-scatter.19
